TPU v7x, 32 devices: a whole 2x2x4 slice. The times are simulated.
32 devices in a mesh: stream: 4 (over y, x), tm: 8 (over z, core).
Axes of the slice: x: 2, y: 2, z: 4, core: 2. Of those that a mesh axis runs over, the one named last changes fastest.
Arguments:
- voltages: float32 [2, 4096, 4096], P(None, ('stream', 'tm')), parts along dimension 1, may hold values from -100 to 100
- taps: float32 [16, 4096], replicated, may hold values from -1.5 to 1.5
- flags: int32 [128], P('stream'), parts along dimension 0, may hold values from 0 to 1, as said below
Outputs:
- dynamic: float32 [1024, 4096], P('stream', 'tm'), parts along dimension 0
- kurtosis: float32 [16384], P(('stream', 'tm')), parts along dimension 0
- spectrum: float32 [16384], P(('stream', 'tm')), parts along dimension 0
There are 4 independent parts, one for each index of `stream`. A program takes and returns all parts, laid end to end along the dimension named above; an argument that names none is the same for every part. Nothing has to cross between parts.
Inputs may be any that keep to these rules, and one draw needn't show every extreme that they name: `flags`: at least one and at most 16 blocks of a stream are flagged.
All inputs are finite; a program needn't handle non-finite values.
Results may differ from a plain program's by a relative error of at most 0.00016.
Values sent between devices are 32-bit elements; how exact they have to be, the bound alone decides.
A program may use at most 64 MiB of HBM per device.

v0:
```python
import math

import jax
import jax.numpy as jnp
from jax import lax
from jax.sharding import PartitionSpec as P

SUMMED = 4


def from_behind(value, axis, by):
    count = lax.axis_size(axis)
    pairs = [(i, i + by) for i in range(count) if 0 <= i + by < count]
    return lax.ppermute(value, axis, pairs)


def rotation(angles):
    cosine = jnp.cos(angles)
    sine = jnp.sin(angles)
    return jnp.stack([jnp.stack([cosine, -sine], 1), jnp.stack([sine, cosine], 1)], 0)


def transform(filtered):
    frames = filtered.shape[1]
    channel_list = filtered.shape[2]
    outer_len = 1
    while 4 * outer_len * outer_len <= channel_list and outer_len < 32:
        outer_len = 2 * outer_len
    inner_len = channel_list // outer_len
    low_index = jnp.arange(outer_len, dtype=jnp.int32)
    high_index = jnp.arange(inner_len, dtype=jnp.int32)
    outer_table = rotation(
        (low_index[:, None] * high_index[None, :] % outer_len).astype(jnp.float32)
        * (2.0 * math.pi / outer_len)
    )
    twist_turn = (high_index[:, None] * high_index[None, :] % channel_list).astype(jnp.float32) * (
        2.0 * math.pi / channel_list
    )
    twist_cos = jnp.cos(twist_turn)
    twist_sin = jnp.sin(twist_turn)
    inner_table = rotation(
        (high_index[:, None] * low_index[None, :] % outer_len).astype(jnp.float32)
        * (2.0 * math.pi / outer_len)
    )
    shaped = filtered.reshape(2, frames, outer_len, inner_len)
    sectioned = jnp.einsum("sfab,satd->tfdb", shaped, outer_table, precision=lax.Precision.HIGHEST)
    twisted_real = sectioned[0] * twist_cos + sectioned[1] * twist_sin
    twisted_imag = sectioned[1] * twist_cos - sectioned[0] * twist_sin
    twisted = jnp.stack([twisted_real, twisted_imag], 0)
    result = jnp.einsum("tfdb,tbuc->ufcd", twisted, inner_table, precision=lax.Precision.HIGHEST)
    return result.reshape(2, frames, channel_list)


def body(voltages, taps, flags):
    frames = voltages.shape[1]
    channel_list = voltages.shape[2]
    tap_count = taps.shape[0]
    groups = lax.axis_size("tm")
    tail_rows = voltages[:, frames - (tap_count - 1) :, :]
    before = from_behind(tail_rows, "tm", 1)
    padded = jnp.concatenate([before, voltages], axis=1)
    filtered = jnp.zeros(voltages.shape, jnp.float32)
    for offset in range(tap_count):
        begin = tap_count - 1 - offset
        filtered = filtered + taps[offset][None, None, :] * padded[:, begin : begin + frames, :]
    spectra = transform(filtered)
    channel_powers = spectra[0] * spectra[0] + spectra[1] * spectra[1]
    block_count = flags.shape[0]
    block_width = channel_list // block_count
    clean_count = jnp.broadcast_to(
        (1 - flags).astype(jnp.float32)[:, None], (block_count, block_width)
    ).reshape(channel_list)
    frame_total = frames * groups
    local_block_width = channel_list // groups
    local_mean_power = lax.axis_index("tm") * local_block_width
    local_clean_count = lax.dynamic_slice_in_dim(clean_count, local_mean_power, local_block_width)
    local_first = jnp.sum(channel_powers, axis=0)
    local_second = jnp.sum(channel_powers * channel_powers, axis=0)
    local_rows = jnp.sum(channel_powers.reshape(frames // SUMMED, SUMMED, channel_list), axis=1)
    local_total = jnp.dot(local_rows, clean_count, precision=lax.Precision.HIGHEST)
    local_dynamic = channel_list * clean_count[None, :] * local_rows / local_total[:, None]
    dynamic = lax.all_to_all(local_dynamic, "tm", split_axis=1, concat_axis=0, tiled=True)
    all_first, all_second = lax.psum((local_first, local_second), "tm")
    group_sum = jnp.dot(all_first, clean_count, precision=lax.Precision.HIGHEST)
    mean_power = lax.dynamic_slice_in_dim(all_first, local_mean_power, local_block_width)
    second_moment = lax.dynamic_slice_in_dim(all_second, local_mean_power, local_block_width)
    kurtosis = (
        (frame_total + 1.0)
        / (frame_total - 1.0)
        * (frame_total * second_moment / (mean_power * mean_power) - 1.0)
    )
    spectrum = channel_list * local_clean_count * mean_power / group_sum
    return (dynamic, kurtosis, spectrum)


def solution(mesh):
    placed = (P(None, ("stream", "tm"), None), P(), P("stream"))
    return jax.shard_map(
        body,
        mesh=mesh,
        in_specs=placed,
        out_specs=(P("stream", "tm"), P(("stream", "tm")), P(("stream", "tm"))),
        check_vma=False,
    )
```

profile of v0, /device:TPU:0, one launch (start us, length us, event | category | flops | bytes accessed | tf_op | source)
XLA Modules:
  0.0 131.1 jit_solution(12339648518364889131)
XLA Ops:
  0.6 1.1 slice.116
  1.7 2.4 %collective-permute-start = (f32[2,15,4096]{2,1,0:T(8,128)S(1)}, f32[2,15,4096]{2,1,0:T(8,128)S(1)}, u32[]{:S(2)}, u32[]{:S(2)}) collective-permute-start(f32[2,15,4096]{2,1,0:T(8,128)S(1)} %slice.116), channel_id=1, source_target_pairs={{0,1},{1,2},{2,3},{3,4},{4,5},{5,6},{6,7},{8,9},{9,10},{10,11},{11... | collective-permute-start | bytes 1474568 | tf_op jit(solution)/shard_map/ppermute | solution.py:14
  4.2 0.1 fusion.78
  4.3 0.3 fusion.64
  4.8 2.6 %fusion.88 = (f32[1,4096]{1,0:T(1,128)S(1)}, f32[1,4096]{1,0:T(1,128)S(1)}, f32[1,4096]{1,0:T(1,128)S(1)}, f32[1,4096]{1,0:T(1,128)S(1)}, f32[1,4096]{1,0:T(1,12...) fusion(f32[16,4096]{1,0:T(8,128)} %param.4), kind=kLoop, calls=%fused_computation.146 | loop fusion | bytes 524288 | tf_op jit(solution)/shard_map/slice | solution.py:65
  7.5 0.7 broadcast_multiply_fusion
  8.3 0.7 subtract_convert_fusion
  9.0 29.5 %fusion.6 = f32[2,128,4096]{2,1,0:T(8,128)S(1)} fusion(f32[2,128,4096]{2,1,0:T(8,128)} %param.3, f32[2,15,4096]{2,1,0:T(8,128)S(1)} %collective-permute-done, f32[4096]{0:T(1024)S(1)} %bitcast.107, f32[4096]{0:T(1024)S(1)} %bitcast.108, f32[4096]{0:T(1024)S(1)} %bitcast.94, f32[4096]{0:T(1024)S(1)} %bitcast.95, f32[4096]{0:T(1024)S(1)} %bitcast.96, ...), kind=kLoop, calls=%fused_computation.38 | loop fusion | flops 48234496 | bytes 9142272 | tf_op jit(solution)/shard_map/add | solution.py:65
  38.5 0.8 copy.34
  39.3 13.9 %convolution_bitcast_fusion = f32[2,128,128,128]{3,2,1,0:T(8,128)S(1)} fusion(f32[1,32,2,128]{3,1,0,2:T(8,128)S(1)} %get-tuple-element.31, f32[1,32,2,128]{3,1,0,2:T(8,128)S(1)} %get-tuple-element.30, f32[2,128,32,128]{3,2,1,0:T(8,128)S(1)} %bitcast.89), kind=kOutput, calls=%fused_computation.20 | convolution fusion | flops 3221241856 | bytes 21037056 | tf_op jit(solution)/shard_map/sfab,satd->tfdb/dot_general | solution.py:46
  53.2 6.9 %multiply_add_fusion = (f32[1,128,128,128]{3,2,1,0:T(8,128)}, f32[1,128,128,128]{3,2,1,0:T(8,128)}) fusion(f32[2,128,128,128]{3,2,1,0:T(8,128)S(1)} %convolution_bitcast_fusion, f32[128,128]{1,0:T(8,128)S(1)} %get-tuple-element.34, f32[128,128]{1,0:T(8,128)S(1)} %get-tuple-element.35), kind=kLoop, calls=%fused_computation.19 | loop fusion | flops 12582912 | bytes 33685504 | tf_op jit(solution)/shard_map/add | solution.py:47
  60.1 18.1 %fusion.49 = f32[2,128,32,128]{3,2,1,0:T(8,128)S(1)} fusion(f32[1,128,2,32]{1,3,0,2:T(8,128)S(1)} %get-tuple-element.29, f32[1,128,2,32]{1,3,0,2:T(8,128)S(1)} %get-tuple-element.28, f32[1,128,128,128]{3,2,1,0:T(8,128)} %get-tuple-element.9, f32[1,128,128,128]{3,2,1,0:T(8,128)} %get-tuple-element.8), kind=kOutput, calls=%fused_computation.82 | convolution fusion | flops 3225436160 | bytes 21037056 | tf_op jit(solution)/shard_map/tfdb,tbuc->ufcd/dot_general | solution.py:50
  78.2 0.6 fusion.86
  78.8 1.8 %add.165 = f32[32,4,4096]{2,1,0:T(4,128)} reshape(f32[1,128,32,128]{3,2,1,0:T(8,128)S(1)} %get-tuple-element.7) | data formatting | bytes 4194304 | tf_op jit(solution)/shard_map/add | solution.py:67
  80.5 2.9 %reduce_sum.33 = f32[32,4096]{1,0:T(8,128)S(1)} reduce(f32[32,4,4096]{2,1,0:T(4,128)} %add.165, f32[]{:T(128)} %constant.57.clone.1), dimensions={1}, to_apply=%region_0.1 | reduce | flops 393216 | bytes 2621444 | tf_op jit(solution)/shard_map/reduce_sum | solution.py:79
  83.4 0.3 copy.35
  83.8 0.5 convolution_bitcast_fusion.1
  84.3 0.1 fusion.53
  84.5 1.1 copy.27
  85.6 9.5 %all-to-all-start = ((f32[32,8,512]{2,0,1:T(8,128)}), f32[32,8,512]{2,0,1:T(8,128)S(1)}, u32[]{:S(2)}, u32[]{:S(2)}) async-start(f32[32,8,512]{2,0,1:T(8,128)} %copy.27), calls=%async_computation | async-start | bytes 1048576 | tf_op jit(solution)/shard_map/all_to_all | solution.py:82
  95.2 33.0 %all-reduce = (f32[4096]{0:T(1024)S(1)}, f32[4096]{0:T(1024)S(1)}) all-reduce(f32[4096]{0:T(1024)S(1)} %bitcast.110, f32[4096]{0:T(1024)S(1)} %bitcast.109), channel_id=1, replica_groups=mesh['stream'=4,'tm'=8] {'tm'}, use_global_device_ids=true, to_apply=%region_2.3 | all-reduce | flops 8192 | bytes 65536 | tf_op jit(solution)/shard_map/psum | solution.py:83
  128.2 0.8 multiply_reduce_fusion.1
  129.0 1.4 %multiply_divide_fusion = (f32[512]{0:T(512)}, f32[512]{0:T(512)}) fusion(f32[4096]{0:T(1024)S(1)} %broadcast_bitcast_fusion, s32[]{:T(128)S(6)} %select_n.82, f32[4096]{0:T(1024)S(1)} %get-tuple-element.6, f32[]{:T(128)} %multiply_reduce_fusion.1, f32[4096]{0:T(1024)S(1)} %get-tuple-element.5), kind=kLoop, calls=%fused_computation.138 | loop fusion | flops 4096 | bytes 10248 | tf_op jit(solution)/shard_map/div | solution.py:92
  130.3 0.8 copy.47
  (12 shorter events, 0.6 us)
Async XLA Ops:
  1.7 7.3 %collective-permute-start = (f32[2,15,4096]{2,1,0:T(8,128)S(1)}, f32[2,15,4096]{2,1,0:T(8,128)S(1)}, u32[]{:S(2)}, u32[]{:S(2)}) collective-permute-start(f32[2,15,4096]{2,1,0:T(8,128)S(1)} %slice.116), channel_id=1, source_target_pairs={{0,1},{1,2},{2,3},{3,4},{4,5},{5,6},{6,7},{8,9},{9,10},{10,11},{11... | collective-permute-start | bytes 1474568 | tf_op jit(solution)/shard_map/ppermute | solution.py:14
  85.6 44.7 %all-to-all-start = ((f32[32,8,512]{2,0,1:T(8,128)}), f32[32,8,512]{2,0,1:T(8,128)S(1)}, u32[]{:S(2)}, u32[]{:S(2)}) async-start(f32[32,8,512]{2,0,1:T(8,128)} %copy.27), calls=%async_computation | async-start | bytes 1048576 | tf_op jit(solution)/shard_map/all_to_all | solution.py:82
where the time goes:
time: 131 us
  other arithmetic  44.1 us (34%)
  blocking collectives  33 us (25%)
  matrix products  32.5 us (25%)
  starting transfers between devices  12 us (9%)
  local copies, waits for them, and re-layouts  8.86 us (7%)
    psum x1, blocking collectives, body(): all_first, all_second = lax.psum((local_first, local_second), 'tm')  33 us
    add x1, other arithmetic, body(): filtered + taps[offset][None, None, :] * padded[:, begin:begin + frames, :]  29.5 us
    dot_general x1, matrix products, transform(): jnp.einsum('tfdb,tbuc->ufcd', twisted, inner_table, precision=lax.Precisi...  18.1 us
    dot_general x1, matrix products, transform(): jnp.einsum('sfab,satd->tfdb', shaped, outer_table, precision=lax.Precisio...  13.9 us
    all_to_all x1, starting transfers between devices, body(): lax.all_to_all(local_dynamic, 'tm', split_axis=1, concat_axis=0, tiled=True)  9.55 us
    add x1, other arithmetic, transform(): twisted_real = sectioned[0] * twist_cos + sectioned[1] * twist_sin  6.94 us
    reduce_sum x1, other arithmetic, body(): jnp.sum(channel_powers.reshape(frames // SUMMED, SUMMED, channel_list), a...  2.88 us
    slice x1, local copies, waits for them, and re-layouts, body(): taps[offset][None, None, :] * padded[:, begin:begin + frames, :]  2.65 us
  transfers between devices with their start and end apart: 2, of which 0 were waited for; matrix products, arithmetic and copies ran while one was open for 5% of the time, Pallas kernels for 0%

commit v1 on v0

v1 whole, which is shorter than its diff:
```python
import functools
import math

import jax
import jax.numpy as jnp
import numpy as np
from jax import lax
from jax.experimental import pallas as pl
from jax.experimental.pallas import tpu as pltpu
from jax.sharding import PartitionSpec as P

SUMMED = 4
LANES = 128
ROWS = 8


def rotate_by(value, k, n):
    re, im = value
    if k == 0:
        return re, im
    if 4 * k == n:
        return im, -re
    half = math.sqrt(0.5)
    if 8 * k == n:
        return (re + im) * half, (im - re) * half
    if 8 * k == 3 * n:
        return (im - re) * half, (re + im) * (-half)
    c = math.cos(2.0 * math.pi * k / n)
    s = math.sin(2.0 * math.pi * k / n)
    return re * c + im * s, im * c - re * s


def fft(values):
    n = len(values)
    if n == 1:
        return values
    even = fft(values[0::2])
    odd = fft(values[1::2])
    low, high = [], []
    for k in range(n // 2):
        tr, ti = rotate_by(odd[k], k, n)
        er, ei = even[k]
        low.append((er + tr, ei + ti))
        high.append((er - tr, ei - ti))
    return low + high


def kernel(n, x_hbm, taps_ref, flags_ref, cos_ref, sin_ref, wa_ref, wb_ref,
           dyn_hbm, kurt_ref, spec_ref,
           xbuf, ybuf, zbuf, m1buf, m2buf, bbuf, tbuf, vbuf, sendbuf, recvbuf,
           load_sem, halo_send, halo_recv, send_sem, recv_sem, out_sem):
    me = lax.axis_index("tm")
    frames, channels = x_hbm.shape[1], x_hbm.shape[2]
    tap_count = taps_ref.shape[0]
    head = xbuf.shape[2] - frames
    outer = channels // LANES
    span = LANES // outer
    step = SUMMED * ROWS
    chunks = frames // step
    part = channels // n
    blocks = flags_ref.shape[0]
    width = channels // blocks

    def load(i, a):
        return pltpu.make_async_copy(
            x_hbm.at[:, pl.ds(i * step, step), pl.ds(pl.multiple_of(a * LANES, LANES), LANES)],
            xbuf.at[:, a, pl.ds(head + i * step, step), :], load_sem.at[i])

    def loaded(i):
        rows = xbuf.at[:, :, pl.ds(head + i * step, step), :]
        pltpu.make_async_copy(rows, rows, load_sem.at[i]).wait()

    for i in range(chunks):
        def start_load(a, carry, i=i):
            load(i, a).start()
            return carry

        lax.fori_loop(0, outer, start_load, 0)

    barrier = pltpu.get_barrier_semaphore()

    def greet(off, carry):
        pl.semaphore_signal(barrier, inc=1, device_id={"tm": lax.rem(me + off, n)},
                            device_id_type=pl.DeviceIdType.MESH)
        return carry

    lax.fori_loop(1, n, greet, 0)
    pl.semaphore_wait(barrier, n - 1)

    def halo(a):
        return pltpu.make_async_remote_copy(
            src_ref=x_hbm.at[:, pl.ds(frames - head, head), pl.ds(pl.multiple_of(a * LANES, LANES), LANES)],
            dst_ref=xbuf.at[:, a, pl.ds(0, head), :],
            send_sem=halo_send, recv_sem=halo_recv,
            device_id={"tm": lax.rem(me + 1, n)}, device_id_type=pl.DeviceIdType.MESH)

    def whole_halo():
        return pltpu.make_async_remote_copy(
            src_ref=xbuf.at[:, :, pl.ds(0, head), :],
            dst_ref=xbuf.at[:, :, pl.ds(0, head), :],
            send_sem=halo_send, recv_sem=halo_recv,
            device_id={"tm": lax.rem(me + 1, n)}, device_id_type=pl.DeviceIdType.MESH)

    @pl.when(me < n - 1)
    def _():
        def start_halo(a, carry):
            halo(a).start()
            return carry

        lax.fori_loop(0, outer, start_halo, 0)

    @pl.when(me == 0)
    def _():
        xbuf[:, :, 0:head, :] = jnp.zeros((2, outer, head, LANES), jnp.float32)

    m1buf[...] = jnp.zeros_like(m1buf)
    m2buf[...] = jnp.zeros_like(m2buf)
    lane = lax.broadcasted_iota(jnp.int32, (1, LANES), 1)
    clean = []
    clean_row = jnp.zeros((1, LANES), jnp.float32)
    for b in range(blocks):
        clean.append((1 - flags_ref[b]).astype(jnp.float32))
        clean_row = jnp.where(lane // (width // outer) == b, clean[b], clean_row)

    def relayout(count):
        for g in range(-(-count * outer // LANES)):
            tbuf[g] = bbuf[g * LANES:(g + 1) * LANES, :].T
        for r in range(count):
            g, place = (r * outer) // LANES, (r * outer) % LANES
            total = None
            for e1 in range(span):
                piece = tbuf[g, pl.ds(e1, outer, stride=span), :]
                shift = (e1 * outer - place) % LANES
                if shift:
                    piece = pltpu.roll(piece, shift, 1)
                total = piece if total is None else jnp.where(lane // outer == e1, piece, total)
            vbuf[r * outer:(r + 1) * outer, :] = total

    def send(first, count, slot, off):
        other = lax.rem(me + off, n)
        return pltpu.make_async_remote_copy(
            src_ref=sendbuf.at[pl.ds(first, count), pl.ds(pl.multiple_of(other * part, LANES), part)],
            dst_ref=recvbuf.at[me, pl.ds(first, count), :],
            send_sem=send_sem.at[slot, off], recv_sem=recv_sem.at[slot, me],
            device_id={"tm": other}, device_id_type=pl.DeviceIdType.MESH)

    def arrival(first, count, slot, source):
        return pltpu.make_async_remote_copy(
            src_ref=sendbuf.at[pl.ds(first, count), pl.ds(0, part)],
            dst_ref=recvbuf.at[source, pl.ds(first, count), :],
            send_sem=send_sem.at[slot, 0], recv_sem=recv_sem.at[slot, source],
            device_id={"tm": source}, device_id_type=pl.DeviceIdType.MESH)

    pieces = []
    order = list(range(1, chunks)) + [0]
    for slot, chunk in enumerate(order):
        if slot == 0:
            loaded(0)
        if chunk:
            loaded(chunk)
        else:
            @pl.when(me > 0)
            def _():
                whole_halo().wait_recv()
        base = head + chunk * step

        def fir(a, carry):
            columns = pl.ds(pl.multiple_of(a * LANES, LANES), LANES)
            coefficients = [jnp.broadcast_to(taps_ref[pl.ds(k, 1), columns], (ROWS, LANES))
                            for k in range(tap_count)]
            for s in range(2):
                sums = [None] * SUMMED
                for o in range(1 - tap_count, SUMMED):
                    value = xbuf[s, a, pl.ds(base + o, ROWS, stride=SUMMED), :]
                    for j in range(SUMMED):
                        if 0 <= j - o < tap_count:
                            term = coefficients[j - o] * value
                            sums[j] = term if sums[j] is None else sums[j] + term
                for j in range(SUMMED):
                    ybuf[s, a, j * ROWS:(j + 1) * ROWS, :] = sums[j]
            return carry

        lax.fori_loop(0, outer, fir, 0)

        def columns_fft(j, carry):
            rows = pl.ds(pl.multiple_of(j * ROWS, ROWS), ROWS)
            result = fft([(ybuf[0, a, rows, :], ybuf[1, a, rows, :]) for a in range(outer)])
            for d in range(outer):
                re, im = result[d]
                c, s = cos_ref[d:d + 1, :], sin_ref[d:d + 1, :]
                zbuf[d, rows, 0:LANES] = re * c + im * s
                zbuf[d, rows, LANES:2 * LANES] = im * c - re * s
            return carry

        lax.fori_loop(0, SUMMED, columns_fft, 0)

        group = 8

        def lanes_dft(g, row_sum):
            z = zbuf[pl.ds(g * group, group), :, :].reshape(group * step, 2 * LANES)
            high = z.astype(jnp.bfloat16)
            low = (z - high.astype(jnp.float32)).astype(jnp.bfloat16)
            y = (jnp.dot(high, wa_ref[...], preferred_element_type=jnp.float32)
                 + jnp.dot(low, wa_ref[...], preferred_element_type=jnp.float32)
                 + jnp.dot(high, wb_ref[...], preferred_element_type=jnp.float32))
            re, im = y[:, :LANES], y[:, LANES:]
            power = re * re + im * im
            for k in range(group):
                piece = [power[k * step + j * ROWS:k * step + (j + 1) * ROWS] for j in range(SUMMED)]
                first = (piece[0] + piece[1]) + (piece[2] + piece[3])
                second = ((piece[0] * piece[0] + piece[1] * piece[1])
                          + (piece[2] * piece[2] + piece[3] * piece[3]))
                d = g * group + k
                bbuf[pl.ds(d, ROWS, stride=outer), :] = first
                m1buf[d] = m1buf[d] + first
                m2buf[d] = m2buf[d] + second
                row_sum = row_sum + first
            return row_sum

        row_sum = lax.fori_loop(0, outer // group, lanes_dft, jnp.zeros((ROWS, LANES), jnp.float32))
        row_total = jnp.sum(row_sum * clean_row, axis=1, keepdims=True)
        scale = channels / row_total
        relayout(ROWS)
        first_row = ROWS * (1 + chunk)
        for q in range(outer):
            tile = vbuf[pl.ds(q, ROWS, stride=outer), :]
            sendbuf[first_row:first_row + ROWS, q * LANES:(q + 1) * LANES] = (
                tile * (scale * clean[q * LANES // width]))
        count = ROWS
        if slot == chunks - 1:
            first = jnp.sum(m1buf[...], axis=1)
            second = jnp.sum(m2buf[...], axis=1)
            bbuf[0:outer, :] = first
            bbuf[outer:2 * outer, :] = second
            bbuf[2 * outer:, :] = jnp.zeros((bbuf.shape[0] - 2 * outer, LANES), jnp.float32)
            relayout(2)
            group_sum = jnp.sum(jnp.sum(first, axis=0, keepdims=True) * clean_row, axis=1, keepdims=True)
            vbuf[2 * outer:3 * outer, :] = jnp.broadcast_to(group_sum, (outer, LANES))
            for q in range(outer):
                sendbuf[0:ROWS, q * LANES:(q + 1) * LANES] = vbuf[pl.ds(q, ROWS, stride=outer), :]
            first_row, count = 0, 2 * ROWS
        pieces.append((first_row, count))

        def start(off, carry, first_row=first_row, count=count, slot=slot):
            send(first_row, count, slot, off).start()
            return carry

        lax.fori_loop(1, n, start, 0)
        recvbuf[me, first_row:first_row + count, :] = sendbuf[
            first_row:first_row + count, pl.ds(pl.multiple_of(me * part, LANES), part)]

    for slot, (first_row, count) in enumerate(pieces):
        def receive(off, carry, first_row=first_row, count=count, slot=slot):
            arrival(first_row, count, slot, lax.rem(me + n - off, n)).wait_recv()
            return carry

        lax.fori_loop(1, n, receive, 0)

    out = pltpu.make_async_copy(recvbuf.at[:, pl.ds(ROWS, chunks * ROWS), :], dyn_hbm, out_sem)
    out.start()
    total = recvbuf[0, 0:ROWS, :]
    for source in range(1, n):
        total = total + recvbuf[source, 0:ROWS, :]
    mean_power, second_moment, whole = total[0:1], total[1:2], total[2:3]
    count = float(frames * n)
    kurt_ref[...] = ((count + 1.0) / (count - 1.0)
                     * (count * second_moment / (mean_power * mean_power) - 1.0))
    own = jnp.zeros((1, part), jnp.float32)
    place = lax.broadcasted_iota(jnp.int32, (1, part), 1) + me * part
    for b in range(blocks):
        own = jnp.where(place // width == b, clean[b], own)
    spec_ref[...] = channels * own * mean_power / whole

    for slot, (first_row, count) in enumerate(pieces):
        def sent(off, carry, first_row=first_row, count=count, slot=slot):
            send(first_row, count, slot, off).wait_send()
            return carry

        lax.fori_loop(1, n, sent, 0)

    @pl.when(me < n - 1)
    def _():
        whole_halo().wait_send()

    out.wait()


def body(n, voltages, taps, flags):
    frames, channels = voltages.shape[1], voltages.shape[2]
    head = -(-(taps.shape[0] - 1) // ROWS) * ROWS
    outer = channels // LANES
    step = SUMMED * ROWS
    chunks = frames // step
    part = channels // n
    turn = 2.0 * np.pi * np.outer(np.arange(outer), np.arange(LANES)) / channels
    angle = 2.0 * np.pi * (np.outer(np.arange(LANES), np.arange(LANES)) % LANES) / LANES
    table = np.block([[np.cos(angle), -np.sin(angle)], [np.sin(angle), np.cos(angle)]]).astype(np.float32)
    table_high = table.astype(jnp.bfloat16)
    table_low = (table - table_high.astype(np.float32)).astype(jnp.bfloat16)
    vmem = pl.BlockSpec(memory_space=pltpu.VMEM)
    dynamic, kurtosis, spectrum = pl.pallas_call(
        functools.partial(kernel, n),
        out_shape=(
            jax.ShapeDtypeStruct((n, chunks * ROWS, part), jnp.float32),
            jax.ShapeDtypeStruct((1, part), jnp.float32),
            jax.ShapeDtypeStruct((1, part), jnp.float32),
        ),
        in_specs=[pl.BlockSpec(memory_space=pl.ANY), vmem, pl.BlockSpec(memory_space=pltpu.SMEM),
                  vmem, vmem, vmem, vmem],
        out_specs=(pl.BlockSpec(memory_space=pl.ANY), vmem, vmem),
        scratch_shapes=[
            pltpu.VMEM((2, outer, head + frames, LANES), jnp.float32),
            pltpu.VMEM((2, outer, step, LANES), jnp.float32),
            pltpu.VMEM((outer, step, 2 * LANES), jnp.float32),
            pltpu.VMEM((outer, ROWS, LANES), jnp.float32),
            pltpu.VMEM((outer, ROWS, LANES), jnp.float32),
            pltpu.VMEM((ROWS * outer, LANES), jnp.float32),
            pltpu.VMEM((ROWS * outer // LANES, LANES, LANES), jnp.float32),
            pltpu.VMEM((ROWS * outer, LANES), jnp.float32),
            pltpu.VMEM(((1 + chunks) * ROWS, channels), jnp.float32),
            pltpu.VMEM((n, (1 + chunks) * ROWS, part), jnp.float32),
            pltpu.SemaphoreType.DMA((chunks,)),
            pltpu.SemaphoreType.DMA,
            pltpu.SemaphoreType.DMA,
            pltpu.SemaphoreType.DMA((chunks, n)),
            pltpu.SemaphoreType.DMA((chunks, n)),
            pltpu.SemaphoreType.DMA,
        ],
        compiler_params=pltpu.CompilerParams(
            collective_id=0, has_side_effects=True, vmem_limit_bytes=40 * 1024 * 1024),
    )(voltages, taps, flags, jnp.asarray(np.cos(turn), jnp.float32), jnp.asarray(np.sin(turn), jnp.float32),
      jnp.asarray(table_high), jnp.asarray(table_low))
    return dynamic.reshape(n * chunks * ROWS, part), kurtosis.reshape(part), spectrum.reshape(part)


def solution(mesh):
    return jax.shard_map(
        functools.partial(body, mesh.shape["tm"]),
        mesh=mesh,
        in_specs=(P(None, ("stream", "tm"), None), P(), P("stream")),
        out_specs=(P("stream", "tm"), P(("stream", "tm")), P(("stream", "tm"))),
        check_vma=False,
    )
```

time: 131 us -> 37.3 us (0.28)
  the two profiles are of different devices: /device:TPU:0 before, /device:TPU:25 now
where the time goes in v1:
time: 37.3 us; the launch traced here: 36.6 us
  Pallas kernels  27 us (72%)
  local copies, waits for them, and re-layouts  8.98 us (24%)
  between operations  0.65 us (2%)
    pallas_call x1, Pallas kernels, body(): pl.pallas_call(functools.partial(kernel, n), out_shape=(jax.ShapeDtypeStr...  27 us
    unnamed x17, local copies, waits for them, and re-layouts  8.98 us

profile of v1, /device:TPU:25, one launch (start us, length us, event | category | flops | bytes accessed | tf_op | source)
XLA Modules:
  0.0 36.6 jit_solution(12205927704345580277)
XLA Ops:
  0.6 0.0 copy-start
  0.6 2.2 %copy-done = f32[2,128,4096]{2,1,0:T(8,128)S(1)} copy-done((f32[2,128,4096]{2,1,0:T(8,128)S(1)}, f32[2,128,4096]{2,1,0:T(8,128)}, u32[]{:S(2)}) %copy-start) | copy-done | bytes 4194328
  2.8 0.0 copy-start.1
  2.8 0.9 %copy-done.1 = f32[16,4096]{1,0:T(8,128)S(1)} copy-done((f32[16,4096]{1,0:T(8,128)S(1)}, f32[16,4096]{1,0:T(8,128)}, u32[]{:S(2)}) %copy-start.1) | copy-done | bytes 262168
  3.8 0.0 copy-start.2
  3.8 0.9 %copy-done.2 = bf16[256,256]{1,0:T(8,128)(2,1)S(1)} copy-done((bf16[256,256]{1,0:T(8,128)(2,1)S(1)}, bf16[256,256]{1,0:T(8,128)(2,1)}, u32[]{:S(2)}) %copy-start.2) | copy-done | bytes 131096
  4.7 0.0 copy-start.3
  4.7 0.9 %copy-done.3 = bf16[256,256]{1,0:T(8,128)(2,1)S(1)} copy-done((bf16[256,256]{1,0:T(8,128)(2,1)S(1)}, bf16[256,256]{1,0:T(8,128)(2,1)}, u32[]{:S(2)}) %copy-start.3) | copy-done | bytes 131096
  5.6 0.0 copy-start.4
  5.6 0.7 %copy-done.4 = f32[32,128]{1,0:T(8,128)S(1)} copy-done((f32[32,128]{1,0:T(8,128)S(1)}, f32[32,128]{1,0:T(8,128)}, u32[]{:S(2)}) %copy-start.4) | copy-done | bytes 16408
  6.3 0.0 copy-start.5
  6.3 0.7 %copy-done.5 = f32[32,128]{1,0:T(8,128)S(1)} copy-done((f32[32,128]{1,0:T(8,128)S(1)}, f32[32,128]{1,0:T(8,128)}, u32[]{:S(2)}) %copy-start.5) | copy-done | bytes 16408
  7.0 0.0 copy-start.6
  7.0 0.7 %copy-done.6 = s32[32]{0:T(128)S(1)} copy-done((s32[32]{0:T(128)S(1)}, s32[32]{0:T(128)}, u32[]{:S(2)}) %copy-start.6) | copy-done | bytes 152
  7.7 27.0 %shard_map.94 = (f32[8,32,512]{2,1,0:T(8,128)S(1)}, f32[1,512]{1,0:T(1,128)S(1)}, f32[1,512]{1,0:T(1,128)S(1)}) custom-call(f32[2,128,4096]{2,1,0:T(8,128)S(1)} %copy-done, f32[16,4096]{1,0:T(8,128)S(1)} %copy-done.1, s32[32]{0:T(128)S(1)} %copy-done.6, f32[32,128]{1,0:T(8,128)S(1)} %copy-done.5, f32[32,128]{1,0:T(8,128)S(1)} %copy-done.4, ...), custom_call_target="tpu_custom_call" | custom-call | tf_op jit(solution)/shard_map/pallas_call | solution.py:301
  34.6 0.8 %copy.13 = f32[256,512]{1,0:T(8,128)} copy(f32[256,512]{1,0:T(8,128)S(1)} %bitcast.3) | data formatting | bytes 1048576
  35.4 0.6 %copy.14 = f32[512]{0:T(512)} copy(f32[512]{0:T(512)S(1)} %bitcast.5) | data formatting | bytes 4096
  36.0 0.6 %copy.15 = f32[512]{0:T(512)} copy(f32[512]{0:T(512)S(1)} %bitcast.4) | data formatting | bytes 4096
Async XLA Ops:
  0.6 2.2 %copy-start = (f32[2,128,4096]{2,1,0:T(8,128)S(1)}, f32[2,128,4096]{2,1,0:T(8,128)}, u32[]{:S(2)}) copy-start(f32[2,128,4096]{2,1,0:T(8,128)} %x_hbm.1) | copy-start | bytes 12582916
  2.8 0.9 %copy-start.1 = (f32[16,4096]{1,0:T(8,128)S(1)}, f32[16,4096]{1,0:T(8,128)}, u32[]{:S(2)}) copy-start(f32[16,4096]{1,0:T(8,128)} %taps_ref.1) | copy-start | bytes 786436
  3.8 0.9 %copy-start.2 = (bf16[256,256]{1,0:T(8,128)(2,1)S(1)}, bf16[256,256]{1,0:T(8,128)(2,1)}, u32[]{:S(2)}) copy-start(bf16[256,256]{1,0:T(8,128)(2,1)} %constant.11.clone.wb_ref) | copy-start | bytes 393220
  4.7 0.9 %copy-start.3 = (bf16[256,256]{1,0:T(8,128)(2,1)S(1)}, bf16[256,256]{1,0:T(8,128)(2,1)}, u32[]{:S(2)}) copy-start(bf16[256,256]{1,0:T(8,128)(2,1)} %constant.10.clone.wa_ref) | copy-start | bytes 393220
  5.6 0.7 %copy-start.4 = (f32[32,128]{1,0:T(8,128)S(1)}, f32[32,128]{1,0:T(8,128)}, u32[]{:S(2)}) copy-start(f32[32,128]{1,0:T(8,128)} %constant.9.clone.sin_ref) | copy-start | bytes 49156
  6.3 0.7 %copy-start.5 = (f32[32,128]{1,0:T(8,128)S(1)}, f32[32,128]{1,0:T(8,128)}, u32[]{:S(2)}) copy-start(f32[32,128]{1,0:T(8,128)} %constant.8.clone.cos_ref) | copy-start | bytes 49156
  7.0 0.7 %copy-start.6 = (s32[32]{0:T(128)S(1)}, s32[32]{0:T(128)}, u32[]{:S(2)}) copy-start(s32[32]{0:T(128)} %flags_ref.1) | copy-start | bytes 388

commit v2 on v1

--- a/solution.py
+++ b/solution.py
@@ -45,9 +45,9 @@
     return low + high
 
 
-def kernel(n, x_hbm, taps_ref, flags_ref, cos_ref, sin_ref, wa_ref, wb_ref,
+def kernel(n, x_hbm, taps_hbm, flags_hbm, turn_hbm, table_hbm,
            dyn_hbm, kurt_ref, spec_ref,
-           xbuf, ybuf, zbuf, m1buf, m2buf, bbuf, tbuf, vbuf, sendbuf, recvbuf,
+           taps_ref, flags_ref, turn_ref, table_ref, side_sem, xbuf, ybuf, zbuf, m1buf, m2buf, bbuf, tbuf, vbuf, sendbuf, recvbuf,
            load_sem, halo_send, halo_recv, send_sem, recv_sem, out_sem):
     me = lax.axis_index("tm")
     frames, channels = x_hbm.shape[1], x_hbm.shape[2]
@@ -70,6 +70,10 @@
         rows = xbuf.at[:, :, pl.ds(head + i * step, step), :]
         pltpu.make_async_copy(rows, rows, load_sem.at[i]).wait()
 
+    sides = [pltpu.make_async_copy(source, target, side_sem.at[i]) for i, (source, target) in enumerate(
+        ((taps_hbm, taps_ref), (flags_hbm, flags_ref), (turn_hbm, turn_ref), (table_hbm, table_ref)))]
+    for side in sides:
+        side.start()
     for i in range(chunks):
         def start_load(a, carry, i=i):
             load(i, a).start()
@@ -113,6 +117,8 @@
     def _():
         xbuf[:, :, 0:head, :] = jnp.zeros((2, outer, head, LANES), jnp.float32)
 
+    for side in sides:
+        side.wait()
     m1buf[...] = jnp.zeros_like(m1buf)
     m2buf[...] = jnp.zeros_like(m2buf)
     lane = lax.broadcasted_iota(jnp.int32, (1, LANES), 1)
@@ -180,14 +186,14 @@
                     ybuf[s, a, j * ROWS:(j + 1) * ROWS, :] = sums[j]
             return carry
 
-        lax.fori_loop(0, outer, fir, 0)
+        lax.fori_loop(0, outer, fir, 0, unroll=2)
 
         def columns_fft(j, carry):
             rows = pl.ds(pl.multiple_of(j * ROWS, ROWS), ROWS)
             result = fft([(ybuf[0, a, rows, :], ybuf[1, a, rows, :]) for a in range(outer)])
             for d in range(outer):
                 re, im = result[d]
-                c, s = cos_ref[d:d + 1, :], sin_ref[d:d + 1, :]
+                c, s = turn_ref[0, d:d + 1, :], turn_ref[1, d:d + 1, :]
                 zbuf[d, rows, 0:LANES] = re * c + im * s
                 zbuf[d, rows, LANES:2 * LANES] = im * c - re * s
             return carry
@@ -200,9 +206,9 @@
             z = zbuf[pl.ds(g * group, group), :, :].reshape(group * step, 2 * LANES)
             high = z.astype(jnp.bfloat16)
             low = (z - high.astype(jnp.float32)).astype(jnp.bfloat16)
-            y = (jnp.dot(high, wa_ref[...], preferred_element_type=jnp.float32)
-                 + jnp.dot(low, wa_ref[...], preferred_element_type=jnp.float32)
-                 + jnp.dot(high, wb_ref[...], preferred_element_type=jnp.float32))
+            y = (jnp.dot(high, table_ref[0], preferred_element_type=jnp.float32)
+                 + jnp.dot(low, table_ref[0], preferred_element_type=jnp.float32)
+                 + jnp.dot(high, table_ref[1], preferred_element_type=jnp.float32))
             re, im = y[:, :LANES], y[:, LANES:]
             power = re * re + im * im
             for k in range(group):
@@ -305,10 +311,14 @@
             jax.ShapeDtypeStruct((1, part), jnp.float32),
             jax.ShapeDtypeStruct((1, part), jnp.float32),
         ),
-        in_specs=[pl.BlockSpec(memory_space=pl.ANY), vmem, pl.BlockSpec(memory_space=pltpu.SMEM),
-                  vmem, vmem, vmem, vmem],
+        in_specs=[pl.BlockSpec(memory_space=pl.ANY)] * 5,
         out_specs=(pl.BlockSpec(memory_space=pl.ANY), vmem, vmem),
         scratch_shapes=[
+            pltpu.VMEM(taps.shape, jnp.float32),
+            pltpu.SMEM(flags.shape, jnp.int32),
+            pltpu.VMEM((2, outer, LANES), jnp.float32),
+            pltpu.VMEM((2, 2 * LANES, 2 * LANES), jnp.bfloat16),
+            pltpu.SemaphoreType.DMA((4,)),
             pltpu.VMEM((2, outer, head + frames, LANES), jnp.float32),
             pltpu.VMEM((2, outer, step, LANES), jnp.float32),
             pltpu.VMEM((outer, step, 2 * LANES), jnp.float32),
@@ -327,9 +337,9 @@
             pltpu.SemaphoreType.DMA,
         ],
         compiler_params=pltpu.CompilerParams(
-            collective_id=0, has_side_effects=True, vmem_limit_bytes=40 * 1024 * 1024),
-    )(voltages, taps, flags, jnp.asarray(np.cos(turn), jnp.float32), jnp.asarray(np.sin(turn), jnp.float32),
-      jnp.asarray(table_high), jnp.asarray(table_low))
+            collective_id=0, has_side_effects=True, vmem_limit_bytes=65000 * 1024),
+    )(voltages, taps, flags, jnp.asarray(np.stack([np.cos(turn), np.sin(turn)]), jnp.float32),
+      jnp.asarray(np.stack([table_high, table_low])))
     return dynamic.reshape(n * chunks * ROWS, part), kurtosis.reshape(part), spectrum.reshape(part)
 
 

time: 37.3 us -> 32.7 us (0.88); the launches traced: 36.6 us -> 32.5 us
  local copies, waits for them, and re-layouts: 8.98 us -> 4.37 us
  Pallas kernels: 27 us -> 27.5 us
    unnamed x17 -> x3, local copies, waits for them, and re-layouts: 8.98 us -> 4.37 us
    pallas_call x1, Pallas kernels: 27 us -> 27.5 us  [body(): pl.pallas_call(functools.partial(kernel, n), out_shape=(jax.ShapeDtypeStr...]
where the time goes in v2:
time: 32.7 us; the launch traced here: 32.5 us
  Pallas kernels  27.5 us (84%)
  local copies, waits for them, and re-layouts  4.37 us (13%)
  between operations  0.64 us (2%)
    pallas_call x1, Pallas kernels, body(): pl.pallas_call(functools.partial(kernel, n), out_shape=(jax.ShapeDtypeStr...  27.5 us
    unnamed x3, local copies, waits for them, and re-layouts  4.37 us

profile of v2, /device:TPU:25, one launch (start us, length us, event | category | flops | bytes accessed | tf_op | source)
XLA Modules:
  0.0 32.5 jit_solution(17198374999005774597)
XLA Ops:
  0.6 27.5 %shard_map.76 = (f32[8,32,512]{2,1,0:T(8,128)}, f32[1,512]{1,0:T(1,128)}, f32[1,512]{1,0:T(1,128)}) custom-call(f32[2,128,4096]{2,1,0:T(8,128)} %x_hbm.1, f32[16,4096]{1,0:T(8,128)} %taps_hbm.1, s32[32]{0:T(128)} %flags_hbm.1, f32[2,32,128]{2,1,0:T(8,128)} %constant.4.clone.turn_hbm, bf16[2,256,256]{2,1,0:T(8,128)(2,1)} %constant.5.clone.table_hbm), custom_call_target="tpu_custom_call" | custom-call | tf_op jit(solution)/shard_map/pallas_call | solution.py:307
  28.1 1.9 %copy.11 = f32[256,512]{1,0:T(8,128)} copy(f32[256,512]{1,0:T(8,128)} %bitcast.3) | data formatting | bytes 1048576
  30.0 1.3 %copy.12 = f32[512]{0:T(512)} copy(f32[512]{0:T(512)} %bitcast.5) | data formatting | bytes 4096
  31.2 1.2 %copy.13 = f32[512]{0:T(512)} copy(f32[512]{0:T(512)} %bitcast.4) | data formatting | bytes 4096

commit v3 on v2

--- a/solution.py
+++ b/solution.py
@@ -46,8 +46,8 @@
 
 
 def kernel(n, x_hbm, taps_hbm, flags_hbm, turn_hbm, table_hbm,
-           dyn_hbm, kurt_ref, spec_ref,
-           taps_ref, flags_ref, turn_ref, table_ref, side_sem, xbuf, ybuf, zbuf, m1buf, m2buf, bbuf, tbuf, vbuf, sendbuf, recvbuf,
+           got_hbm,
+           taps_ref, flags_ref, turn_ref, table_ref, side_sem, xbuf, ybuf, zbuf, m1buf, m2buf, pbuf, bbuf, tbuf, vbuf, sendbuf, recvbuf,
            load_sem, halo_send, halo_recv, send_sem, recv_sem, out_sem):
     me = lax.axis_index("tm")
     frames, channels = x_hbm.shape[1], x_hbm.shape[2]
@@ -176,11 +176,11 @@
                             for k in range(tap_count)]
             for s in range(2):
                 sums = [None] * SUMMED
-                for o in range(1 - tap_count, SUMMED):
-                    value = xbuf[s, a, pl.ds(base + o, ROWS, stride=SUMMED), :]
+                for o in range(1 - tap_count, (SUMMED - 1) * ROWS + 1):
+                    value = xbuf[s, a, pl.ds(base + o, ROWS), :]
                     for j in range(SUMMED):
-                        if 0 <= j - o < tap_count:
-                            term = coefficients[j - o] * value
+                        if 0 <= j * ROWS - o < tap_count:
+                            term = coefficients[j * ROWS - o] * value
                             sums[j] = term if sums[j] is None else sums[j] + term
                 for j in range(SUMMED):
                     ybuf[s, a, j * ROWS:(j + 1) * ROWS, :] = sums[j]
@@ -211,8 +211,9 @@
                  + jnp.dot(high, table_ref[1], preferred_element_type=jnp.float32))
             re, im = y[:, :LANES], y[:, LANES:]
             power = re * re + im * im
+            pbuf[...] = power
             for k in range(group):
-                piece = [power[k * step + j * ROWS:k * step + (j + 1) * ROWS] for j in range(SUMMED)]
+                piece = [pbuf[pl.ds(k * step + j, ROWS, stride=SUMMED), :] for j in range(SUMMED)]
                 first = (piece[0] + piece[1]) + (piece[2] + piece[3])
                 second = ((piece[0] * piece[0] + piece[1] * piece[1])
                           + (piece[2] * piece[2] + piece[3] * piece[3]))
@@ -262,20 +263,8 @@
 
         lax.fori_loop(1, n, receive, 0)
 
-    out = pltpu.make_async_copy(recvbuf.at[:, pl.ds(ROWS, chunks * ROWS), :], dyn_hbm, out_sem)
+    out = pltpu.make_async_copy(recvbuf, got_hbm, out_sem)
     out.start()
-    total = recvbuf[0, 0:ROWS, :]
-    for source in range(1, n):
-        total = total + recvbuf[source, 0:ROWS, :]
-    mean_power, second_moment, whole = total[0:1], total[1:2], total[2:3]
-    count = float(frames * n)
-    kurt_ref[...] = ((count + 1.0) / (count - 1.0)
-                     * (count * second_moment / (mean_power * mean_power) - 1.0))
-    own = jnp.zeros((1, part), jnp.float32)
-    place = lax.broadcasted_iota(jnp.int32, (1, part), 1) + me * part
-    for b in range(blocks):
-        own = jnp.where(place // width == b, clean[b], own)
-    spec_ref[...] = channels * own * mean_power / whole
 
     for slot, (first_row, count) in enumerate(pieces):
         def sent(off, carry, first_row=first_row, count=count, slot=slot):
@@ -289,6 +278,44 @@
         whole_halo().wait_send()
 
     out.wait()
+
+
+def finish(n, got_hbm, flags_hbm, dyn_hbm, kurt_hbm, spec_hbm, got, flags_ref, result, sem):
+    moments = pltpu.make_async_copy(got_hbm.at[:, pl.ds(0, ROWS), :], got.at[:, pl.ds(0, ROWS), :], sem.at[0])
+    rows = pltpu.make_async_copy(
+        got_hbm.at[:, pl.ds(ROWS, got.shape[1] - ROWS), :], got.at[:, pl.ds(ROWS, got.shape[1] - ROWS), :], sem.at[1])
+    side = pltpu.make_async_copy(flags_hbm, flags_ref, sem.at[2])
+    moments.start()
+    side.start()
+    rows.start()
+    moments.wait()
+    side.wait()
+    part = got.shape[2]
+    channels = part * n
+    blocks = flags_ref.shape[0]
+    width = channels // blocks
+    total = got[0, 0:ROWS, :]
+    for source in range(1, n):
+        total = total + got[source, 0:ROWS, :]
+    mean_power, second_moment, whole = total[0:1], total[1:2], total[2:3]
+    count = float((got.shape[1] - ROWS) * SUMMED * n)
+    own = jnp.zeros((1, part), jnp.float32)
+    place = lax.broadcasted_iota(jnp.int32, (1, part), 1) + lax.axis_index("tm") * part
+    for b in range(blocks):
+        own = jnp.where(place // width == b, (1 - flags_ref[b]).astype(jnp.float32), own)
+    result[0] = ((count + 1.0) / (count - 1.0)
+                 * (count * second_moment / (mean_power * mean_power) - 1.0))
+    result[1] = channels * own * mean_power / whole
+    kurt = pltpu.make_async_copy(result.at[0], kurt_hbm, sem.at[0])
+    spec = pltpu.make_async_copy(result.at[1], spec_hbm, sem.at[2])
+    kurt.start()
+    spec.start()
+    rows.wait()
+    dyn = pltpu.make_async_copy(got.at[:, pl.ds(ROWS, got.shape[1] - ROWS), :], dyn_hbm, sem.at[1])
+    dyn.start()
+    kurt.wait()
+    spec.wait()
+    dyn.wait()
 
 
 def body(n, voltages, taps, flags):
@@ -303,16 +330,11 @@
     table = np.block([[np.cos(angle), -np.sin(angle)], [np.sin(angle), np.cos(angle)]]).astype(np.float32)
     table_high = table.astype(jnp.bfloat16)
     table_low = (table - table_high.astype(np.float32)).astype(jnp.bfloat16)
-    vmem = pl.BlockSpec(memory_space=pltpu.VMEM)
-    dynamic, kurtosis, spectrum = pl.pallas_call(
+    got = pl.pallas_call(
         functools.partial(kernel, n),
-        out_shape=(
-            jax.ShapeDtypeStruct((n, chunks * ROWS, part), jnp.float32),
-            jax.ShapeDtypeStruct((1, part), jnp.float32),
-            jax.ShapeDtypeStruct((1, part), jnp.float32),
-        ),
+        out_shape=jax.ShapeDtypeStruct((n, (1 + chunks) * ROWS, part), jnp.float32),
         in_specs=[pl.BlockSpec(memory_space=pl.ANY)] * 5,
-        out_specs=(pl.BlockSpec(memory_space=pl.ANY), vmem, vmem),
+        out_specs=pl.BlockSpec(memory_space=pl.ANY),
         scratch_shapes=[
             pltpu.VMEM(taps.shape, jnp.float32),
             pltpu.SMEM(flags.shape, jnp.int32),
@@ -324,6 +346,7 @@
             pltpu.VMEM((outer, step, 2 * LANES), jnp.float32),
             pltpu.VMEM((outer, ROWS, LANES), jnp.float32),
             pltpu.VMEM((outer, ROWS, LANES), jnp.float32),
+            pltpu.VMEM((8 * step, LANES), jnp.float32),
             pltpu.VMEM((ROWS * outer, LANES), jnp.float32),
             pltpu.VMEM((ROWS * outer // LANES, LANES, LANES), jnp.float32),
             pltpu.VMEM((ROWS * outer, LANES), jnp.float32),
@@ -340,6 +363,23 @@
             collective_id=0, has_side_effects=True, vmem_limit_bytes=65000 * 1024),
     )(voltages, taps, flags, jnp.asarray(np.stack([np.cos(turn), np.sin(turn)]), jnp.float32),
       jnp.asarray(np.stack([table_high, table_low])))
+    dynamic, kurtosis, spectrum = pl.pallas_call(
+        functools.partial(finish, n),
+        out_shape=(
+            jax.ShapeDtypeStruct((n, chunks * ROWS, part), jnp.float32),
+            jax.ShapeDtypeStruct((1, part), jnp.float32),
+            jax.ShapeDtypeStruct((1, part), jnp.float32),
+        ),
+        in_specs=[pl.BlockSpec(memory_space=pl.ANY)] * 2,
+        out_specs=[pl.BlockSpec(memory_space=pl.ANY)] * 3,
+        scratch_shapes=[
+            pltpu.VMEM((n, (1 + chunks) * ROWS, part), jnp.float32),
+            pltpu.SMEM(flags.shape, jnp.int32),
+            pltpu.VMEM((2, 1, part), jnp.float32),
+            pltpu.SemaphoreType.DMA((3,)),
+        ],
+        compiler_params=pltpu.CompilerParams(vmem_limit_bytes=65000 * 1024),
+    )(got, flags)
     return dynamic.reshape(n * chunks * ROWS, part), kurtosis.reshape(part), spectrum.reshape(part)
 
 

time: 32.7 us -> 29.7 us (0.908)
  local copies, waits for them, and re-layouts: 4.37 us -> 0 us
  Pallas kernels: 27.5 us -> 28.9 us
    unnamed x3 -> x0, local copies, waits for them, and re-layouts: 4.37 us -> none
    pallas_call x1 -> x2, Pallas kernels: 27.5 us -> 28.9 us  [the longest x1 27 us: body(): pl.pallas_call(functools.partial(kernel, n), out_shape=jax.ShapeDtypeStru...]
where the time goes in v3:
time: 29.7 us; the launch traced here: 29.5 us
  Pallas kernels  28.9 us (97%)
  between operations  0.64 us (2%)
    pallas_call x1, Pallas kernels, body(): pl.pallas_call(functools.partial(kernel, n), out_shape=jax.ShapeDtypeStru...  27 us
    pallas_call x1, Pallas kernels, body(): pl.pallas_call(functools.partial(finish, n), out_shape=(jax.ShapeDtypeStr...  1.94 us

profile of v3, /device:TPU:25, one launch (start us, length us, event | category | flops | bytes accessed | tf_op | source)
XLA Modules:
  0.0 29.5 jit_solution(17178717591729266785)
XLA Ops:
  0.6 27.0 %shard_map.76.got_hbm = f32[8,40,512]{2,1,0:T(8,128)} custom-call(f32[2,128,4096]{2,1,0:T(8,128)} %x_hbm.1, f32[16,4096]{1,0:T(8,128)} %taps_hbm.1, s32[32]{0:T(128)} %flags_hbm.3, f32[2,32,128]{2,1,0:T(8,128)} %constant.4.clone.turn_hbm, bf16[2,256,256]{2,1,0:T(8,128)(2,1)} %constant.5.clone.table_hbm), custom_call_target="tpu_custom_call" | custom-call | tf_op jit(solution)/shard_map/pallas_call | solution.py:333
  27.6 1.9 %shard_map.77 = (f32[8,32,512]{2,1,0:T(8,128)}, f32[1,512]{1,0:T(1,128)}, f32[1,512]{1,0:T(1,128)}) custom-call(f32[8,40,512]{2,1,0:T(8,128)} %shard_map.76.got_hbm, s32[32]{0:T(128)} %flags_hbm.3), custom_call_target="tpu_custom_call" | custom-call | tf_op jit(solution)/shard_map/pallas_call | solution.py:366
